TPU v7x, 32 devices: a whole 2x2x4 slice. The times are simulated.
32 devices in a mesh: parts: 2 (over y), shot: 4 (over z), freq: 2 (over x), rep: 2 (over core).
Axes of the slice: x: 2, y: 2, z: 4, core: 2. Of those that a mesh axis runs over, the one named last changes fastest.
Arguments:
- recorded: bfloat16 [2, 4, 2048, 2048], P(None, ('parts', 'freq'), ('shot', 'rep')), parts along dimension 1, may hold values from -6 to 6
- receiver_x: float32 [4096], P('parts'), parts along dimension 0, may hold values from -12800 to 12800
- source_x: float32 [4096], P('parts'), parts along dimension 0, may hold values from -12800 to 12800
Outputs:
- predicted: bfloat16 [2, 4, 2048, 2048], P(None, ('parts', 'freq'), ('shot', 'rep')), parts along dimension 1
There are 2 independent parts, one for each index of `parts`. A program takes and returns all parts, laid end to end along the dimension named above; each array names one. Nothing has to cross between parts.
All inputs are finite; a program needn't handle non-finite values.
Results may differ from a plain program's by a relative error of at most 0.013.
Values may be sent and summed in bfloat16 or wider, within the bound.
A program may use at most 64 MiB of HBM per device.

v0:
```python
import functools
import math

import jax
import jax.numpy as jnp
from jax import lax
from jax.experimental import pallas as pl
from jax.experimental.pallas import tpu as pltpu
from jax.sharding import PartitionSpec as P

NSLOW = 1024

two_pi = 6.283185307179586
base_hertz = 40.0
step_hertz = 0.5
slow_max = 0.0005
GROUP = ("shot", "rep")


def angle_table(omega, positions):
    half = NSLOW // 2
    fine = math.gcd(half, 16)
    unit = (omega * (slow_max / NSLOW)) * positions
    coarse = (jnp.arange(half // fine, dtype=jnp.int32) * (2 * fine)).astype(jnp.float32)[:, None] * unit
    small = (2 * jnp.arange(fine, dtype=jnp.int32) + 1).astype(jnp.float32)[:, None] * unit
    cos_a, sin_a = jnp.cos(coarse)[:, None], jnp.sin(coarse)[:, None]
    cos_b, sin_b = jnp.cos(small)[None], jnp.sin(small)[None]
    cosine = cos_a * cos_b - sin_a * sin_b
    sine = sin_a * cos_b + cos_a * sin_b
    return jnp.stack([cosine, sine]).astype(jnp.bfloat16).reshape(NSLOW, positions.shape[0])


def product(form, left, right):
    return jnp.einsum(form, left, right, preferred_element_type=jnp.float32)


def one_frequency(data, receiver_x, source_x, omega):
    shots = data.shape[1]
    src_count, rec_count = source_x.shape[0], receiver_x.shape[0]
    receiver = angle_table(omega, receiver_x)
    source = angle_table(omega, source_x)
    first = lax.axis_index(GROUP) * shots
    mine = angle_table(omega, lax.dynamic_slice_in_dim(source_x, first, shots, 0))
    spread = (product("csr,jr->csj", data, receiver) * math.sqrt(2.0 / rec_count)).astype(jnp.bfloat16)
    met = lax.all_to_all(spread, GROUP, split_axis=2, concat_axis=1, tiled=True)
    plane = (product("qs,csj->cqj", source, met) * math.sqrt(2.0 / src_count)).astype(jnp.bfloat16)
    planes = lax.all_gather(plane, GROUP, axis=2, tiled=True)
    sign = jnp.where(jnp.arange(NSLOW) < NSLOW // 2, 1.0, -1.0) * math.sqrt(2.0 / NSLOW)
    half_way = (product("qs,cqj->csj", mine, planes) * sign).astype(jnp.bfloat16)
    back_real = product("sm,mj->sj", half_way[0], planes[0]) - product("sm,mj->sj", half_way[1], planes[1])
    back_imaginary = product("sm,mj->sj", half_way[0], planes[1]) + product("sm,mj->sj", half_way[1], planes[0])
    back = (jnp.stack([back_real, back_imaginary]) * math.sqrt(1.0 / NSLOW)).astype(jnp.bfloat16)
    return (product("csj,jr->csr", back, receiver) * math.sqrt(2.0 / NSLOW)).astype(jnp.bfloat16)


FINE = 16
HALF = NSLOW // 2
COARSE = HALF // FINE
MESH = pl.DeviceIdType.MESH


def fill_factors(omega, positions, factors):
    count = positions.shape[1]
    tile = math.gcd(count, 256)
    sines = [(-1.0) ** n / math.factorial(2 * n + 1) for n in range(7)]
    cosines = [(-1.0) ** n / math.factorial(2 * n) for n in range(8)]
    turn_high = 6.28125
    turn_low = two_pi - turn_high

    def step(i, carry):
        lanes = pl.ds(pl.multiple_of(i * tile, tile), tile)
        unit = positions[:, lanes] * (omega * (slow_max / NSLOW))
        row = lax.broadcasted_iota(jnp.int32, (COARSE + FINE, tile), 0)
        steps = jnp.where(row < COARSE, row * (2 * FINE), 2 * (row - COARSE) + 1).astype(jnp.float32)
        phase = steps * unit
        turns = jnp.floor(phase * (1.0 / two_pi) + 0.5)
        half = 0.5 * ((phase - turns * turn_high) - turns * turn_low)
        square = half * half
        sine, cosine = sines[-1], cosines[-1]
        for term in reversed(sines[:-1]):
            sine = sine * square + term
        for term in reversed(cosines[:-1]):
            cosine = cosine * square + term
        sine = sine * half
        factors[0, :, lanes] = 1.0 - 2.0 * sine * sine
        factors[1, :, lanes] = 2.0 * sine * cosine
        return carry

    lax.fori_loop(0, count // tile, step, 0)


def fill_table(factors, table):
    count = table.shape[1]
    tile = math.gcd(count, 512)
    for first in range(0, count, tile):
        lanes = slice(first, first + tile)
        cos_b = factors[0, COARSE : COARSE + FINE, lanes]
        sin_b = factors[1, COARSE : COARSE + FINE, lanes]

        def step(a, carry):
            cos_a = factors[0, pl.ds(a, 1), lanes]
            sin_a = factors[1, pl.ds(a, 1), lanes]
            row = pl.multiple_of(a * FINE, FINE)
            table[pl.ds(row, FINE), lanes] = (cos_a * cos_b - sin_a * sin_b).astype(jnp.bfloat16)
            table[pl.ds(HALF + row, FINE), lanes] = (sin_a * cos_b + cos_a * sin_b).astype(jnp.bfloat16)
            return carry

        lax.fori_loop(0, COARSE, step, 0, unroll=4)


def dot(left, right):
    return jnp.dot(left, right, preferred_element_type=jnp.float32)


def whole_kernel(
    chips, first_hertz, data, receiver_x, source_x, back, kept,
    receiver, source, receiver_f, source_f, mine, outgoing, met, planes, half_way,
    spread_send, spread_recv, plane_send, plane_recv, kept_sem,
):
    cores = 2
    group = chips * cores
    width = NSLOW // group
    shots = data.shape[0] // 2
    z, c = lax.axis_index("shot"), lax.axis_index("rep")
    me = z * cores + c

    def place(d):
        return {"shot": d // cores, "rep": d % cores}

    barrier = pltpu.get_barrier_semaphore()
    for d in range(group):
        @pl.when(d != me)
        def _():
            pl.semaphore_signal(barrier, inc=1, device_id=place(d), device_id_type=MESH)

    hertz = first_hertz(lax.axis_index("freq")).astype(jnp.float32)
    omega = two_pi * (base_hertz + step_hertz * hertz)
    fill_factors(omega, receiver_x, receiver_f)
    fill_table(receiver_f, receiver)
    pl.semaphore_wait(barrier, group - 1)

    def spread_copy(h, d):
        return pltpu.make_async_remote_copy(
            src_ref=outgoing.at[h, d], dst_ref=met.at[h, pl.ds(pl.multiple_of(me * shots, shots), shots)],
            send_sem=spread_send.at[h, d], recv_sem=spread_recv.at[h, me],
            device_id=place(d), device_id_type=MESH,
        )

    scale = math.sqrt(2.0 / data.shape[1])
    order = sorted(range(1, chips), key=lambda k: abs(2 * k - chips)) + [0]
    for h in range(2):
        for offset in order:
            target = lax.rem(z + offset, chips)
            rows = receiver[pl.ds(pl.multiple_of(target * (cores * width), cores * width), cores * width), :]
            part = lax.dot_general(
                data[h * shots : (h + 1) * shots, :], rows, (((1,), (1,)), ((), ())),
                preferred_element_type=jnp.float32,
            )
            part = (part * scale).astype(jnp.bfloat16)
            for e in range(cores):
                d = target * cores + e
                piece = part[:, e * width : (e + 1) * width]
                if offset == 0:
                    @pl.when(d == me)
                    def _():
                        met[h, pl.ds(pl.multiple_of(me * shots, shots), shots), :] = piece

                    @pl.when(d != me)
                    def _():
                        outgoing[h, d] = piece
                        spread_copy(h, d).start()
                else:
                    outgoing[h, d] = piece
                    spread_copy(h, d).start()

    keep = pltpu.make_async_copy(receiver, kept, kept_sem)
    keep.start()

    fill_factors(omega, source_x, source_f)
    fill_table(source_f, source)
    local = source[:, pl.ds(pl.multiple_of(me * shots, shots), shots)]
    mine[...] = local.T

    def plane_copy(way, h, d):
        to = [{"shot": z + 1, "rep": c}, {"shot": z - 1, "rep": c}, {"shot": z, "rep": 1 - c}][way]
        piece = planes.at[d, :, h * width : (h + 1) * width]
        return pltpu.make_async_remote_copy(
            src_ref=piece, dst_ref=piece, send_sem=plane_send.at[way, h, d], recv_sem=plane_recv.at[h, d],
            device_id=to, device_id_type=MESH,
        )

    scale = math.sqrt(2.0 / source.shape[1])
    tile = 256
    more_up, more_down = z < chips - 1, z > 0
    for h in range(2):
        for d in range(group):
            @pl.when(d != me)
            def _():
                pltpu.make_async_remote_copy(
                    src_ref=outgoing.at[h, d], dst_ref=met.at[h, pl.ds(d * shots, shots)],
                    send_sem=spread_send.at[h, d], recv_sem=spread_recv.at[h, d],
                    device_id=place(d), device_id_type=MESH,
                ).wait_recv()

        def plane_rows(i, carry):
            rows = pl.ds(pl.multiple_of(i * tile, tile), tile)
            piece = (dot(source[rows, :], met[h]) * scale).astype(jnp.bfloat16)
            planes[me, rows, h * width : (h + 1) * width] = piece
            return carry

        lax.fori_loop(0, NSLOW // tile, plane_rows, 0)

        @pl.when(more_up)
        def _():
            plane_copy(0, h, me).start()

        @pl.when(more_down)
        def _():
            plane_copy(1, h, me).start()

        plane_copy(2, h, me).start()

    def half_slice(d):
        sign = (1 - 2 * (d // (group // 2))).astype(jnp.float32)
        part = (dot(mine[...], planes[d]) * math.sqrt(2.0 / NSLOW) * sign).astype(jnp.bfloat16)
        lanes = pl.ds(pl.multiple_of(d * width, width), width)
        half_way[:shots, lanes] = part[:, :width]
        half_way[shots:, lanes] = part[:, width:]

    half_slice(me)
    for k in range(1, chips):
        for h in range(2):
            for way, sign in ((0, -1), (1, 1)):
                origin = z + sign * k

                @pl.when((origin >= 0) & (origin < chips))
                def _():
                    d = origin * cores + c
                    plane_copy(2, h, d).wait_recv()

                    @pl.when((more_up, more_down)[way])
                    def _():
                        plane_copy(way, h, d).start()

                    plane_copy(2, h, d).start()
                    if h == 1:
                        half_slice(d)

        for sign in ((-1, 1) if k > 1 else (1,)):
            origin = z + sign * (k - 1)

            @pl.when((origin >= 0) & (origin < chips))
            def _():
                d = origin * cores + 1 - c
                plane_copy(2, 0, d).wait_recv()
                plane_copy(2, 1, d).wait_recv()
                half_slice(d)

    for sign in (-1, 1):
        origin = z + sign * (chips - 1)

        @pl.when((origin >= 0) & (origin < chips))
        def _():
            d = origin * cores + 1 - c
            plane_copy(2, 0, d).wait_recv()
            plane_copy(2, 1, d).wait_recv()
            half_slice(d)

    scale_back = math.sqrt(1.0 / NSLOW)

    def back_slice(d, carry):
        both = dot(half_way[...], planes[d])
        lanes = pl.ds(pl.multiple_of(d * width, width), width)
        back[:shots, lanes] = ((both[:shots, :width] - both[shots:, width:]) * scale_back).astype(jnp.bfloat16)
        back[shots:, lanes] = ((both[:shots, width:] + both[shots:, :width]) * scale_back).astype(jnp.bfloat16)
        return carry

    lax.fori_loop(0, group, back_slice, 0)
    keep.wait()
    for h in range(2):
        for d in range(group):
            @pl.when(d != me)
            def _():
                spread_copy(h, d).wait_send()
        plane_copy(2, h, me).wait_send()

        @pl.when(more_up)
        def _():
            plane_copy(0, h, me).wait_send()

        @pl.when(more_down)
        def _():
            plane_copy(1, h, me).wait_send()

        for k in range(1, chips):
            for way, sign in ((0, -1), (1, 1)):
                origin = z + sign * k

                @pl.when((origin >= 0) & (origin < chips))
                def _():
                    d = origin * cores + c

                    @pl.when((more_up, more_down)[way])
                    def _():
                        plane_copy(way, h, d).wait_send()

                    plane_copy(2, h, d).wait_send()


def one_frequency_fused(chips, first_hertz, data, receiver_x, source_x):
    shots, rec_count = data.shape[1:]
    src_count = source_x.shape[0]
    group = 2 * chips
    width = NSLOW // group
    vmem = pl.BlockSpec(memory_space=pltpu.VMEM)
    half = jnp.bfloat16
    back, receiver = pl.pallas_call(
        functools.partial(whole_kernel, chips, first_hertz),
        out_shape=(
            jax.ShapeDtypeStruct((2 * shots, NSLOW), half),
            jax.ShapeDtypeStruct((NSLOW, rec_count), half),
        ),
        in_specs=[vmem] * 3,
        out_specs=(vmem, pl.BlockSpec(memory_space=pl.ANY)),
        scratch_shapes=[
            pltpu.VMEM((NSLOW, rec_count), half),
            pltpu.VMEM((NSLOW, src_count), half),
            pltpu.VMEM((2, COARSE + FINE, rec_count), jnp.float32),
            pltpu.VMEM((2, COARSE + FINE, src_count), jnp.float32),
            pltpu.VMEM((shots, NSLOW), half),
            pltpu.VMEM((2, group, shots, width), half),
            pltpu.VMEM((2, src_count, width), half),
            pltpu.VMEM((group, NSLOW, 2 * width), half),
            pltpu.VMEM((2 * shots, NSLOW), half),
            pltpu.SemaphoreType.DMA((2, group)),
            pltpu.SemaphoreType.DMA((2, group)),
            pltpu.SemaphoreType.DMA((3, 2, group)),
            pltpu.SemaphoreType.DMA((2, group)),
            pltpu.SemaphoreType.DMA,
        ],
        compiler_params=pltpu.CompilerParams(
            collective_id=0, has_side_effects=True, vmem_limit_bytes=60 * 1024 * 1024
        ),
        name="plane_wave_multiples",
    )(data.reshape(2 * shots, rec_count), receiver_x.reshape(1, rec_count), source_x.reshape(1, src_count))
    result = (dot(back, receiver) * math.sqrt(2.0 / NSLOW)).astype(half)
    return result.reshape(2, shots, rec_count)


def fits(mesh_shape, shots):
    group = mesh_shape["shot"] * mesh_shape["rep"]
    return mesh_shape["rep"] == 2 and NSLOW % (128 * group) == 0 and shots % 128 == 0


def body(chips, fused, recorded, receiver_x, source_x):
    per_device = recorded.shape[1]
    first_freq = lax.axis_index("freq") * per_device
    outs = []
    for k in range(per_device):
        omega = two_pi * (base_hertz + step_hertz * (first_freq + k).astype(jnp.float32))
        if fused(recorded.shape[2]):
            first_hertz = functools.partial(lambda k, f: f * per_device + k, k)
            outs.append(one_frequency_fused(chips, first_hertz, recorded[:, k], receiver_x, source_x))
        else:
            outs.append(one_frequency(recorded[:, k], receiver_x, source_x, omega))
    return jnp.stack(outs, axis=1)


def solution(mesh):
    return jax.shard_map(
        functools.partial(body, mesh.shape["shot"], functools.partial(fits, mesh.shape)),
        mesh=mesh,
        in_specs=(P(None, ("parts", "freq"), ("shot", "rep"), None), P("parts"), P("parts")),
        out_specs=P(None, ("parts", "freq"), ("shot", "rep"), None),
        check_vma=False,
    )
```

profile of v0, /device:TPU:0, one launch (start us, length us, event | category | flops | bytes accessed | tf_op | source)
XLA Modules:
  0.0 76.0 jit_solution(14691916894093547634)
XLA Ops:
  0.0 69.8 %plane_wave_multiples.1 = (bf16[512,1024]{1,0:T(8,128)(2,1)}, bf16[1024,2048]{1,0:T(8,128)(2,1)}) custom-call(bf16[512,2048]{1,0:T(8,128)(2,1)} %bitcast.8, f32[1,2048]{1,0:T(1,128)} %bitcast.9, f32[1,2048]{1,0:T(1,128)} %bitcast.10), custom_call_target="tpu_custom_call" | custom-call | tf_op jit(solution)/shard_map/plane_wave_multiples/pallas_call | solution.py:317
  69.8 6.2 %multiply_convert_fusion = bf16[512,2048]{1,0:T(8,128)(2,1)} fusion(bf16[512,1024]{1,0:T(8,128)(2,1)} %get-tuple-element.7, bf16[1024,2048]{1,0:T(8,128)(2,1)} %get-tuple-element.8), kind=kOutput, calls=%fused_computation | convolution fusion | flops 2149580800 | bytes 7340032 | tf_op jit(solution)/shard_map/dot_general | solution.py:112
where the time goes:
time: 76.1 us; the launch traced here: 76 us
  Pallas kernels  69.8 us (92%)
  matrix products  6.17 us (8%)
    pallas_call x1, Pallas kernels, one_frequency_fused(): pl.pallas_call(functools.partial(whole_kernel, chips, first_hertz), out_s...  69.8 us
    dot_general x1, matrix products, dot(): return jnp.dot(left, right, preferred_element_type=jnp.float32)  6.17 us

commit v1 on v0

--- a/solution.py
+++ b/solution.py
@@ -113,9 +113,9 @@
 
 
 def whole_kernel(
-    chips, first_hertz, data, receiver_x, source_x, back, kept,
-    receiver, source, receiver_f, source_f, mine, outgoing, met, planes, half_way,
-    spread_send, spread_recv, plane_send, plane_recv, kept_sem,
+    chips, first_hertz, data_in, receiver_in, source_in, back, receiver,
+    data, receiver_x, source_x, source, receiver_f, source_f, mine, outgoing, met, planes, half_way,
+    spread_send, spread_recv, plane_send, plane_recv, load_sem,
 ):
     cores = 2
     group = chips * cores
@@ -123,6 +123,12 @@
     shots = data.shape[0] // 2
     z, c = lax.axis_index("shot"), lax.axis_index("rep")
     me = z * cores + c
+    loads = [
+        pltpu.make_async_copy(src, dst, load_sem.at[i])
+        for i, (src, dst) in enumerate(((receiver_in, receiver_x), (source_in, source_x), (data_in, data)))
+    ]
+    for load in loads:
+        load.start()
 
     def place(d):
         return {"shot": d // cores, "rep": d % cores}
@@ -135,8 +141,10 @@
 
     hertz = first_hertz(lax.axis_index("freq")).astype(jnp.float32)
     omega = two_pi * (base_hertz + step_hertz * hertz)
+    loads[0].wait()
     fill_factors(omega, receiver_x, receiver_f)
     fill_table(receiver_f, receiver)
+    loads[2].wait()
     pl.semaphore_wait(barrier, group - 1)
 
     def spread_copy(h, d):
@@ -173,9 +181,7 @@
                     outgoing[h, d] = piece
                     spread_copy(h, d).start()
 
-    keep = pltpu.make_async_copy(receiver, kept, kept_sem)
-    keep.start()
-
+    loads[1].wait()
     fill_factors(omega, source_x, source_f)
     fill_table(source_f, source)
     local = source[:, pl.ds(pl.multiple_of(me * shots, shots), shots)]
@@ -276,7 +282,6 @@
         return carry
 
     lax.fori_loop(0, group, back_slice, 0)
-    keep.wait()
     for h in range(2):
         for d in range(group):
             @pl.when(d != me)
@@ -320,10 +325,12 @@
             jax.ShapeDtypeStruct((2 * shots, NSLOW), half),
             jax.ShapeDtypeStruct((NSLOW, rec_count), half),
         ),
-        in_specs=[vmem] * 3,
-        out_specs=(vmem, pl.BlockSpec(memory_space=pl.ANY)),
+        in_specs=[pl.BlockSpec(memory_space=pltpu.HBM)] * 3,
+        out_specs=(vmem, vmem),
         scratch_shapes=[
-            pltpu.VMEM((NSLOW, rec_count), half),
+            pltpu.VMEM((2 * shots, rec_count), half),
+            pltpu.VMEM((1, rec_count), jnp.float32),
+            pltpu.VMEM((1, src_count), jnp.float32),
             pltpu.VMEM((NSLOW, src_count), half),
             pltpu.VMEM((2, COARSE + FINE, rec_count), jnp.float32),
             pltpu.VMEM((2, COARSE + FINE, src_count), jnp.float32),
@@ -336,13 +343,16 @@
             pltpu.SemaphoreType.DMA((2, group)),
             pltpu.SemaphoreType.DMA((3, 2, group)),
             pltpu.SemaphoreType.DMA((2, group)),
-            pltpu.SemaphoreType.DMA,
+            pltpu.SemaphoreType.DMA((3,)),
         ],
         compiler_params=pltpu.CompilerParams(
-            collective_id=0, has_side_effects=True, vmem_limit_bytes=60 * 1024 * 1024
+            collective_id=0, has_side_effects=True, vmem_limit_bytes=26 * 1024 * 1024
         ),
         name="plane_wave_multiples",
-    )(data.reshape(2 * shots, rec_count), receiver_x.reshape(1, rec_count), source_x.reshape(1, src_count))
+    )(*[
+        pltpu.with_memory_space_constraint(x, pltpu.HBM)
+        for x in (data.reshape(2 * shots, rec_count), receiver_x.reshape(1, rec_count), source_x.reshape(1, src_count))
+    ])
     result = (dot(back, receiver) * math.sqrt(2.0 / NSLOW)).astype(half)
     return result.reshape(2, shots, rec_count)
 

time: 76.1 us -> 71.7 us (0.942)
  matrix products: 6.17 us -> 3.66 us
  Pallas kernels: 69.8 us -> 67.9 us
    dot_general x1, matrix products: 6.17 us -> 3.66 us  [dot(): return jnp.dot(left, right, preferred_element_type=jnp.float32)]
    pallas_call x1, Pallas kernels: 69.8 us -> 67.9 us  [one_frequency_fused(): pl.pallas_call(functools.partial(whole_kernel, chips, first_hertz), out_s...]
where the time goes in v1:
time: 71.7 us; the launch traced here: 71.5 us
  Pallas kernels  67.9 us (95%)
  matrix products  3.66 us (5%)
    pallas_call x1, Pallas kernels, one_frequency_fused(): pl.pallas_call(functools.partial(whole_kernel, chips, first_hertz), out_s...  67.9 us
    dot_general x1, matrix products, dot(): return jnp.dot(left, right, preferred_element_type=jnp.float32)  3.66 us

profile of v1, /device:TPU:0, one launch (start us, length us, event | category | flops | bytes accessed | tf_op | source)
XLA Modules:
  0.0 71.5 jit_solution(3831723835817709652)
XLA Ops:
  0.0 67.9 %plane_wave_multiples.1 = (bf16[512,1024]{1,0:T(8,128)(2,1)S(1)}, bf16[1024,2048]{1,0:T(8,128)(2,1)S(1)}) custom-call(bf16[512,2048]{1,0:T(8,128)(2,1)} %bitcast.8, f32[1,2048]{1,0:T(1,128)} %bitcast.9, f32[1,2048]{1,0:T(1,128)} %bitcast.10), custom_call_target="tpu_custom_call" | custom-call | tf_op jit(solution)/shard_map/plane_wave_multiples/pallas_call | solution.py:322
  67.9 3.7 %multiply_convert_fusion = bf16[512,2048]{1,0:T(8,128)(2,1)} fusion(bf16[512,1024]{1,0:T(8,128)(2,1)S(1)} %get-tuple-element.7, bf16[1024,2048]{1,0:T(8,128)(2,1)S(1)} %get-tuple-element.8), kind=kOutput, calls=%fused_computation | convolution fusion | flops 2149580800 | bytes 7340032 | tf_op jit(solution)/shard_map/dot_general | solution.py:112

commit v2 on v1

v2 whole, which is shorter than its diff:
```python
import functools
import math

import jax
import jax.numpy as jnp
from jax import lax
from jax.experimental import pallas as pl
from jax.experimental.pallas import tpu as pltpu
from jax.sharding import PartitionSpec as P

NSLOW = 1024

two_pi = 6.283185307179586
base_hertz = 40.0
step_hertz = 0.5
slow_max = 0.0005
GROUP = ("shot", "rep")


def angle_table(omega, positions):
    half = NSLOW // 2
    fine = math.gcd(half, 16)
    unit = (omega * (slow_max / NSLOW)) * positions
    coarse = (jnp.arange(half // fine, dtype=jnp.int32) * (2 * fine)).astype(jnp.float32)[:, None] * unit
    small = (2 * jnp.arange(fine, dtype=jnp.int32) + 1).astype(jnp.float32)[:, None] * unit
    cos_a, sin_a = jnp.cos(coarse)[:, None], jnp.sin(coarse)[:, None]
    cos_b, sin_b = jnp.cos(small)[None], jnp.sin(small)[None]
    cosine = cos_a * cos_b - sin_a * sin_b
    sine = sin_a * cos_b + cos_a * sin_b
    return jnp.stack([cosine, sine]).astype(jnp.bfloat16).reshape(NSLOW, positions.shape[0])


def product(form, left, right):
    return jnp.einsum(form, left, right, preferred_element_type=jnp.float32)


def one_frequency(data, receiver_x, source_x, omega):
    shots = data.shape[1]
    src_count, rec_count = source_x.shape[0], receiver_x.shape[0]
    receiver = angle_table(omega, receiver_x)
    source = angle_table(omega, source_x)
    first = lax.axis_index(GROUP) * shots
    mine = angle_table(omega, lax.dynamic_slice_in_dim(source_x, first, shots, 0))
    spread = (product("csr,jr->csj", data, receiver) * math.sqrt(2.0 / rec_count)).astype(jnp.bfloat16)
    met = lax.all_to_all(spread, GROUP, split_axis=2, concat_axis=1, tiled=True)
    plane = (product("qs,csj->cqj", source, met) * math.sqrt(2.0 / src_count)).astype(jnp.bfloat16)
    planes = lax.all_gather(plane, GROUP, axis=2, tiled=True)
    sign = jnp.where(jnp.arange(NSLOW) < NSLOW // 2, 1.0, -1.0) * math.sqrt(2.0 / NSLOW)
    half_way = (product("qs,cqj->csj", mine, planes) * sign).astype(jnp.bfloat16)
    back_real = product("sm,mj->sj", half_way[0], planes[0]) - product("sm,mj->sj", half_way[1], planes[1])
    back_imaginary = product("sm,mj->sj", half_way[0], planes[1]) + product("sm,mj->sj", half_way[1], planes[0])
    back = (jnp.stack([back_real, back_imaginary]) * math.sqrt(1.0 / NSLOW)).astype(jnp.bfloat16)
    return (product("csj,jr->csr", back, receiver) * math.sqrt(2.0 / NSLOW)).astype(jnp.bfloat16)


FINE = 16
HALF = NSLOW // 2
COARSE = HALF // FINE
BLOCK = 128
PAIRS = HALF // BLOCK
PIECES = 4
MESH = pl.DeviceIdType.MESH

OWNER = (1, 2, 0, 3, 1, 2, 0, 3)
OWN = tuple(tuple(nb for nb, owner in enumerate(OWNER) if owner == at) for at in range(4))
ORDER = (
    (2, 0, 6, 4, 1, 5, 3, 7),
    (0, 4, 1, 2, 5, 6, 3, 7),
    (1, 5, 0, 3, 4, 7, 2, 6),
    (3, 1, 7, 5, 0, 4, 2, 6),
)
BLOCKS = len(OWNER)


def fill_factors(omega, positions, factors, first, rows):
    count = positions.shape[1]
    tile = math.gcd(count, 256)
    sines = [(-1.0) ** n / math.factorial(2 * n + 1) for n in range(7)]
    cosines = [(-1.0) ** n / math.factorial(2 * n) for n in range(8)]
    turn_high = 6.28125
    turn_low = two_pi - turn_high

    def step(i, carry):
        lanes = pl.ds(pl.multiple_of(i * tile, tile), tile)
        unit = positions[:, lanes] * (omega * (slow_max / NSLOW))
        row = lax.broadcasted_iota(jnp.int32, (rows, tile), 0) + first
        steps = jnp.where(row < FINE, 2 * row + 1, (row - FINE) * (2 * FINE)).astype(jnp.float32)
        phase = steps * unit
        turns = jnp.floor(phase * (1.0 / two_pi) + 0.5)
        half = 0.5 * ((phase - turns * turn_high) - turns * turn_low)
        square = half * half
        sine, cosine = sines[-1], cosines[-1]
        for term in reversed(sines[:-1]):
            sine = sine * square + term
        for term in reversed(cosines[:-1]):
            cosine = cosine * square + term
        sine = sine * half
        factors[0, first : first + rows, lanes] = 1.0 - 2.0 * sine * sine
        factors[1, first : first + rows, lanes] = 2.0 * sine * cosine
        return carry

    lax.fori_loop(0, count // tile, step, 0)


def fill_pair(factors, table, p):
    count = table.shape[1]
    tile = math.gcd(count, 512)
    steps = BLOCK // FINE
    for first in range(0, count, tile):
        lanes = slice(first, first + tile)
        cos_b = factors[0, :FINE, lanes]
        sin_b = factors[1, :FINE, lanes]

        def step(a, carry):
            cos_a = factors[0, pl.ds(FINE + p * steps + a, 1), lanes]
            sin_a = factors[1, pl.ds(FINE + p * steps + a, 1), lanes]
            row = pl.multiple_of(2 * BLOCK * p + a * FINE, FINE)
            table[pl.ds(row, FINE), lanes] = (cos_a * cos_b - sin_a * sin_b).astype(jnp.bfloat16)
            table[pl.ds(row + BLOCK, FINE), lanes] = (sin_a * cos_b + cos_a * sin_b).astype(jnp.bfloat16)
            return carry

        lax.fori_loop(0, steps, step, 0, unroll=4)


def dot(left, right):
    return jnp.dot(left, right, preferred_element_type=jnp.float32)


def whole_kernel(
    first_hertz, data_in, receiver_in, source_in, back, receiver,
    data, receiver_x, source_x, source, receiver_f, source_f, mine, outgoing, met, planes, half_way, total,
    spread_send, spread_recv, plane_send, plane_recv, twin_recv, load_sem,
):
    chips, cores = len(OWN), 2
    group = chips * cores
    shots = data.shape[0] // 2
    z, c = lax.axis_index("shot"), lax.axis_index("rep")
    me = z * cores + c
    side = z // 2
    more_up, more_down = z < chips - 1, z > 0

    def pick(values):
        out = jnp.int32(values[-1])
        for i, value in enumerate(values[:-1]):
            out = jnp.where(z == i, jnp.int32(value), out)
        return out

    packed = pick([sum(nb << (3 * i) for i, nb in enumerate(row)) for row in ORDER])

    def nth(i):
        return lax.rem(packed >> (3 * i), BLOCKS)

    def place(d):
        return {"shot": d // cores, "rep": d % cores}

    loads = [
        pltpu.make_async_copy(src, dst, load_sem.at[i])
        for i, (src, dst) in enumerate(((receiver_in, receiver_x), (data_in, data), (source_in, source_x)))
    ]
    for load in loads:
        load.start()
    barrier = pltpu.get_barrier_semaphore()
    for d in range(group):
        @pl.when(d != me)
        def _():
            pl.semaphore_signal(barrier, inc=1, device_id=place(d), device_id_type=MESH)

    hertz = first_hertz(lax.axis_index("freq")).astype(jnp.float32)
    omega = two_pi * (base_hertz + step_hertz * hertz)
    own_rows = pl.ds(pl.multiple_of(me * shots, shots), shots)

    def spread_copy(p, s, h, to):
        return pltpu.make_async_remote_copy(
            src_ref=outgoing.at[4 * p + 2 * s + h], dst_ref=met.at[p, own_rows],
            send_sem=spread_send, recv_sem=spread_recv.at[p],
            device_id={"shot": to, "rep": h}, device_id_type=MESH,
        )

    def put(p, h, part):
        part = (part * math.sqrt(2.0 / data.shape[1])).astype(jnp.bfloat16)
        for s in range(2):
            piece = part[:, s * BLOCK : (s + 1) * BLOCK]
            here = me == OWNER[2 * p + s] * cores + h

            @pl.when(here)
            def _():
                met[p, own_rows, :] = piece

            @pl.when(jnp.logical_not(here))
            def _():
                outgoing[4 * p + 2 * s + h] = piece

    def send(p, h):
        for k in range(2):
            s = lax.rem(1 - side + c + k, 2)
            to = jnp.where(s == 0, OWNER[2 * p], OWNER[2 * p + 1])

            @pl.when((to != z) | (c != h))
            def _():
                spread_copy(p, s, h, to).start()

    def spread(p, rows):
        return lax.dot_general(
            data[rows, :], receiver[2 * BLOCK * p : 2 * BLOCK * (p + 1), :], (((1,), (1,)), ((), ())),
            preferred_element_type=jnp.float32,
        )

    loads[0].wait()
    first_rows = FINE + BLOCK // FINE
    fill_factors(omega, receiver_x, receiver_f, 0, first_rows)
    fill_pair(receiver_f, receiver, 0)
    loads[1].wait()
    for h in range(2):
        put(0, h, spread(0, slice(h * shots, (h + 1) * shots)))
        if h == 0:
            pl.semaphore_wait(barrier, group - 1)
        send(0, h)
    fill_factors(omega, receiver_x, receiver_f, first_rows, FINE + COARSE - first_rows)
    for p in range(1, PAIRS):
        fill_pair(receiver_f, receiver, p)
        part = spread(p, slice(0, 2 * shots))
        for h in range(2):
            put(p, h, part[h * shots : (h + 1) * shots])
        for h in range(2):
            send(p, h)

    loads[2].wait()
    fill_factors(omega, source_x, source_f, 0, FINE + COARSE)
    for p in range(PAIRS):
        fill_pair(source_f, source, p)
    mine[...] = source[:, own_rows].T
    half_way[...] = jnp.zeros_like(half_way)

    rows_of = NSLOW // PIECES

    def plane_copy(way, nb, h, piece):
        to = [{"shot": z + 1, "rep": c}, {"shot": z - 1, "rep": c}, {"shot": z, "rep": 1 - c}][way]
        part = planes.at[nb, h, pl.ds(pl.multiple_of(piece * rows_of, rows_of), rows_of)]
        return pltpu.make_async_remote_copy(
            src_ref=part, dst_ref=part, send_sem=plane_send.at[way],
            recv_sem=twin_recv.at[nb] if way == 2 else plane_recv.at[nb, piece],
            device_id=to, device_id_type=MESH,
        )

    def whole_copy(way, blocks, recv_sem):
        part = planes.at[blocks, 0]
        return pltpu.make_async_remote_copy(
            src_ref=part, dst_ref=part, send_sem=plane_send.at[way], recv_sem=recv_sem,
            device_id={"rep": 1 - c}, device_id_type=MESH,
        )

    def each_way(nb, up, down, piece, act):
        @pl.when(up)
        def _():
            act(plane_copy(0, nb, c, piece))

        @pl.when(down)
        def _():
            act(plane_copy(1, nb, c, piece))

        act(plane_copy(2, nb, c, piece))

    def start(copy):
        copy.start()

    def own_slice(nb):
        p = nb // 2
        arrived = met.at[p, pl.ds(0, (group - 1) * shots)]
        pltpu.make_async_remote_copy(
            src_ref=arrived, dst_ref=arrived, send_sem=spread_send, recv_sem=spread_recv.at[p],
            device_id={"rep": 1 - c}, device_id_type=MESH,
        ).wait_recv()

        def rows_step(i, carry):
            rows = pl.ds(pl.multiple_of(i * rows_of, rows_of), rows_of)
            piece = (dot(source[rows, :], met[p]) * math.sqrt(2.0 / source.shape[1])).astype(jnp.bfloat16)
            planes[nb, c, rows, :] = piece
            each_way(nb, more_up, more_down, i, start)
            return carry

        lax.fori_loop(0, PIECES, rows_step, 0)

    def ways(i):
        up = pick([int(OWNER[row[i]] < at and at < chips - 1) for at, row in enumerate(ORDER)]) == 1
        down = pick([int(OWNER[row[i]] > at and at > 0) for at, row in enumerate(ORDER)]) == 1
        return up, down

    def passed_slice(i, nb):
        up, down = ways(i)

        def step(piece, carry):
            plane_copy(0, nb, c, piece).wait_recv()
            each_way(nb, up, down, piece, start)
            return carry

        lax.fori_loop(0, PIECES, step, 0)

    def columns(nb):
        return pl.ds(pl.multiple_of(nb * BLOCK, BLOCK), BLOCK)

    def half_slice(nb):
        whole_copy(2, pl.ds(nb, 1), twin_recv.at[nb]).wait_recv()
        sign = (1 - 2 * lax.rem(nb, 2)).astype(jnp.float32) * math.sqrt(2.0 / NSLOW)
        both = jnp.concatenate([planes[nb, 0], planes[nb, 1]], axis=1)
        part = (dot(mine[...], both) * sign).astype(jnp.bfloat16)
        half_way[:shots, columns(nb)] = part[:, :BLOCK]
        half_way[shots:, columns(nb)] = part[:, BLOCK:]

    def mix(both):
        real = both[:shots, :BLOCK] - both[shots:, BLOCK:]
        return real, both[:shots, BLOCK:] + both[shots:, :BLOCK]

    def back_new(nb):
        both = jnp.concatenate([planes[nb, 0], planes[nb, 1]], axis=1)
        return mix(dot(half_way[...], both))

    def back_more(nb, late):
        both = jnp.concatenate([planes[nb, 0, columns(late), :], planes[nb, 1, columns(late), :]], axis=1)
        real, imaginary = mix(dot(half_way[:, columns(late)], both))
        return total[nb, :shots] + real, total[nb, shots:] + imaginary

    def keep_total(nb, parts):
        total[nb, :shots] = parts[0]
        total[nb, shots:] = parts[1]

    def keep_back(nb, parts):
        back[:shots, columns(nb)] = (parts[0] * math.sqrt(1.0 / NSLOW)).astype(jnp.bfloat16)
        back[shots:, columns(nb)] = (parts[1] * math.sqrt(1.0 / NSLOW)).astype(jnp.bfloat16)

    def add_late(n, keep, unroll):
        late = nth(n)

        def step(i, carry):
            keep(nth(i), back_more(nth(i), late))
            return carry

        if n > 0:
            lax.fori_loop(0, n, step, 0, unroll=unroll)
        keep(late, back_new(late))

    for i in range(BLOCKS):
        nb = nth(i)
        owners = [row[i] in own for row, own in zip(ORDER, OWN)]
        mine_now = pick([int(x) for x in owners]) == 1
        if any(owners):
            @pl.when(mine_now)
            def _():
                own_slice(nb)
        if not all(owners):
            @pl.when(jnp.logical_not(mine_now))
            def _():
                passed_slice(i, nb)
        if 0 < i < BLOCKS - 1:
            half_slice(nth(i - 1))
            add_late(i - 1, keep_total, 1)
        if i == BLOCKS - 2:
            half_slice(nb)
            add_late(i, keep_total, 1)

    sent = outgoing.at[pl.ds(0, 2 * BLOCKS - len(OWN[0]))]
    pltpu.make_async_remote_copy(
        src_ref=sent, dst_ref=sent, send_sem=spread_send, recv_sem=spread_recv.at[0],
        device_id={"rep": 1 - c}, device_id_type=MESH,
    ).wait_send()
    half_slice(nth(BLOCKS - 1))
    add_late(BLOCKS - 1, keep_back, True)
    for at in range(chips):
        counts = [sum(owner <= at for owner in OWNER), sum(owner >= at for owner in OWNER)]

        @pl.when(z == at)
        def _():
            for way, count in enumerate(counts):
                if count < BLOCKS:
                    whole_copy(way, pl.ds(0, count), twin_recv.at[0]).wait_send()

    whole_copy(2, pl.ds(0, BLOCKS), twin_recv.at[0]).wait_send()


def one_frequency_fused(first_hertz, data, receiver_x, source_x):
    shots, rec_count = data.shape[1:]
    src_count = source_x.shape[0]
    group = 2 * len(OWN)
    vmem = pl.BlockSpec(memory_space=pltpu.VMEM)
    half = jnp.bfloat16
    back, receiver = pl.pallas_call(
        functools.partial(whole_kernel, first_hertz),
        out_shape=(
            jax.ShapeDtypeStruct((2 * shots, NSLOW), half),
            jax.ShapeDtypeStruct((NSLOW, rec_count), half),
        ),
        in_specs=[pl.BlockSpec(memory_space=pltpu.HBM)] * 3,
        out_specs=(vmem, vmem),
        scratch_shapes=[
            pltpu.VMEM((2 * shots, rec_count), half),
            pltpu.VMEM((1, rec_count), jnp.float32),
            pltpu.VMEM((1, src_count), jnp.float32),
            pltpu.VMEM((NSLOW, src_count), half),
            pltpu.VMEM((2, COARSE + FINE, rec_count), jnp.float32),
            pltpu.VMEM((2, COARSE + FINE, src_count), jnp.float32),
            pltpu.VMEM((shots, NSLOW), half),
            pltpu.VMEM((2 * BLOCKS, shots, BLOCK), half),
            pltpu.VMEM((PAIRS, src_count, BLOCK), half),
            pltpu.VMEM((BLOCKS, 2, NSLOW, BLOCK), half),
            pltpu.VMEM((2 * shots, NSLOW), half),
            pltpu.VMEM((BLOCKS, 2 * shots, BLOCK), jnp.float32),
            pltpu.SemaphoreType.DMA,
            pltpu.SemaphoreType.DMA((PAIRS,)),
            pltpu.SemaphoreType.DMA((3,)),
            pltpu.SemaphoreType.DMA((BLOCKS, PIECES)),
            pltpu.SemaphoreType.DMA((BLOCKS,)),
            pltpu.SemaphoreType.DMA((3,)),
        ],
        compiler_params=pltpu.CompilerParams(
            collective_id=0, has_side_effects=True, vmem_limit_bytes=30 * 1024 * 1024
        ),
        name="plane_wave_multiples",
    )(*[
        pltpu.with_memory_space_constraint(x, pltpu.HBM)
        for x in (data.reshape(2 * shots, rec_count), receiver_x.reshape(1, rec_count), source_x.reshape(1, src_count))
    ])
    result = (dot(back, receiver) * math.sqrt(2.0 / NSLOW)).astype(half)
    return result.reshape(2, shots, rec_count)


def fits(mesh_shape, shots):
    line = mesh_shape["shot"] == len(OWN) and mesh_shape["rep"] == 2
    return line and NSLOW == BLOCKS * BLOCK and shots % 128 == 0


def body(fused, recorded, receiver_x, source_x):
    per_device = recorded.shape[1]
    first_freq = lax.axis_index("freq") * per_device
    outs = []
    for k in range(per_device):
        omega = two_pi * (base_hertz + step_hertz * (first_freq + k).astype(jnp.float32))
        if fused(recorded.shape[2]):
            first_hertz = functools.partial(lambda k, f: f * per_device + k, k)
            outs.append(one_frequency_fused(first_hertz, recorded[:, k], receiver_x, source_x))
        else:
            outs.append(one_frequency(recorded[:, k], receiver_x, source_x, omega))
    return jnp.stack(outs, axis=1)


def solution(mesh):
    return jax.shard_map(
        functools.partial(body, functools.partial(fits, mesh.shape)),
        mesh=mesh,
        in_specs=(P(None, ("parts", "freq"), ("shot", "rep"), None), P("parts"), P("parts")),
        out_specs=P(None, ("parts", "freq"), ("shot", "rep"), None),
        check_vma=False,
    )
```

time: 71.7 us -> 66.1 us (0.922)
  Pallas kernels: 67.9 us -> 61.8 us
    pallas_call x1, Pallas kernels: 67.9 us -> 61.8 us  [one_frequency_fused(): pl.pallas_call(functools.partial(whole_kernel, first_hertz), out_shape=(j...]
where the time goes in v2:
time: 66.1 us; the launch traced here: 65.5 us
  Pallas kernels  61.8 us (93%)
  matrix products  3.66 us (6%)
    pallas_call x1, Pallas kernels, one_frequency_fused(): pl.pallas_call(functools.partial(whole_kernel, first_hertz), out_shape=(j...  61.8 us
    dot_general x1, matrix products, dot(): return jnp.dot(left, right, preferred_element_type=jnp.float32)  3.66 us

profile of v2, /device:TPU:0, one launch (start us, length us, event | category | flops | bytes accessed | tf_op | source)
XLA Modules:
  0.0 65.5 jit_solution(10051030448101050488)
XLA Ops:
  0.0 61.8 %plane_wave_multiples.1 = (bf16[512,1024]{1,0:T(8,128)(2,1)S(1)}, bf16[1024,2048]{1,0:T(8,128)(2,1)S(1)}) custom-call(bf16[512,2048]{1,0:T(8,128)(2,1)} %bitcast.8, f32[1,2048]{1,0:T(1,128)} %bitcast.9, f32[1,2048]{1,0:T(1,128)} %bitcast.10), custom_call_target="tpu_custom_call" | custom-call | tf_op jit(solution)/shard_map/plane_wave_multiples/pallas_call | solution.py:385
  61.8 3.7 %multiply_convert_fusion = bf16[512,2048]{1,0:T(8,128)(2,1)} fusion(bf16[512,1024]{1,0:T(8,128)(2,1)S(1)} %get-tuple-element.7, bf16[1024,2048]{1,0:T(8,128)(2,1)S(1)} %get-tuple-element.8), kind=kOutput, calls=%fused_computation | convolution fusion | flops 2149580800 | bytes 7340032 | tf_op jit(solution)/shard_map/dot_general | solution.py:126

commit v3 on v2

--- a/solution.py
+++ b/solution.py
@@ -61,18 +61,18 @@
 PIECES = 4
 MESH = pl.DeviceIdType.MESH
 
-OWNER = (1, 2, 0, 3, 1, 2, 0, 3)
+OWNER = tuple(2 * s + p % 2 for p in range(PAIRS) for s in range(2))
 OWN = tuple(tuple(nb for nb, owner in enumerate(OWNER) if owner == at) for at in range(4))
 ORDER = (
-    (2, 0, 6, 4, 1, 5, 3, 7),
-    (0, 4, 1, 2, 5, 6, 3, 7),
-    (1, 5, 0, 3, 4, 7, 2, 6),
-    (3, 1, 7, 5, 0, 4, 2, 6),
+    (0, 2, 4, 6, 1, 5, 3, 7),
+    (2, 6, 1, 0, 5, 4, 3, 7),
+    (1, 5, 2, 3, 6, 7, 0, 4),
+    (3, 1, 7, 5, 2, 6, 0, 4),
 )
 BLOCKS = len(OWNER)
 
 
-def fill_factors(omega, positions, factors, first, rows):
+def fill_factors(omega, positions, factors, fine, first, rows):
     count = positions.shape[1]
     tile = math.gcd(count, 256)
     sines = [(-1.0) ** n / math.factorial(2 * n + 1) for n in range(7)]
@@ -83,8 +83,8 @@
     def step(i, carry):
         lanes = pl.ds(pl.multiple_of(i * tile, tile), tile)
         unit = positions[:, lanes] * (omega * (slow_max / NSLOW))
-        row = lax.broadcasted_iota(jnp.int32, (rows, tile), 0) + first
-        steps = jnp.where(row < FINE, 2 * row + 1, (row - FINE) * (2 * FINE)).astype(jnp.float32)
+        row = lax.broadcasted_iota(jnp.int32, (fine + rows, tile), 0)
+        steps = jnp.where(row < fine, 2 * row + 1, (row - fine + first) * (2 * FINE)).astype(jnp.float32)
         phase = steps * unit
         turns = jnp.floor(phase * (1.0 / two_pi) + 0.5)
         half = 0.5 * ((phase - turns * turn_high) - turns * turn_low)
@@ -95,8 +95,10 @@
         for term in reversed(cosines[:-1]):
             cosine = cosine * square + term
         sine = sine * half
-        factors[0, first : first + rows, lanes] = 1.0 - 2.0 * sine * sine
-        factors[1, first : first + rows, lanes] = 2.0 * sine * cosine
+        for i, values in enumerate((1.0 - 2.0 * sine * sine, 2.0 * sine * cosine)):
+            if fine:
+                factors[i, :fine, lanes] = values[:fine]
+            factors[i, pl.ds(FINE + first, rows), lanes] = values[fine:]
         return carry
 
     lax.fori_loop(0, count // tile, step, 0)
@@ -132,6 +134,7 @@
     spread_send, spread_recv, plane_send, plane_recv, twin_recv, load_sem,
 ):
     chips, cores = len(OWN), 2
+    coarse = BLOCK // FINE
     group = chips * cores
     shots = data.shape[0] // 2
     z, c = lax.axis_index("shot"), lax.axis_index("rep")
@@ -180,7 +183,7 @@
         part = (part * math.sqrt(2.0 / data.shape[1])).astype(jnp.bfloat16)
         for s in range(2):
             piece = part[:, s * BLOCK : (s + 1) * BLOCK]
-            here = me == OWNER[2 * p + s] * cores + h
+            here = me == (2 * s + lax.rem(p, 2)) * cores + h
 
             @pl.when(here)
             def _():
@@ -193,7 +196,7 @@
     def send(p, h):
         for k in range(2):
             s = lax.rem(1 - side + c + k, 2)
-            to = jnp.where(s == 0, OWNER[2 * p], OWNER[2 * p + 1])
+            to = 2 * s + lax.rem(p, 2)
 
             @pl.when((to != z) | (c != h))
             def _():
@@ -201,22 +204,22 @@
 
     def spread(p, rows):
         return lax.dot_general(
-            data[rows, :], receiver[2 * BLOCK * p : 2 * BLOCK * (p + 1), :], (((1,), (1,)), ((), ())),
+            data[rows, :], receiver[pl.ds(pl.multiple_of(2 * BLOCK * p, 2 * BLOCK), 2 * BLOCK), :], (((1,), (1,)), ((), ())),
             preferred_element_type=jnp.float32,
         )
 
     loads[0].wait()
-    first_rows = FINE + BLOCK // FINE
-    fill_factors(omega, receiver_x, receiver_f, 0, first_rows)
-    fill_pair(receiver_f, receiver, 0)
+    fill_factors(omega, receiver_x, receiver_f, FINE, side * coarse, coarse)
+    fill_pair(receiver_f, receiver, side)
     loads[1].wait()
     for h in range(2):
-        put(0, h, spread(0, slice(h * shots, (h + 1) * shots)))
+        put(side, h, spread(side, slice(h * shots, (h + 1) * shots)))
         if h == 0:
             pl.semaphore_wait(barrier, group - 1)
-        send(0, h)
-    fill_factors(omega, receiver_x, receiver_f, first_rows, FINE + COARSE - first_rows)
-    for p in range(1, PAIRS):
+        send(side, h)
+    fill_factors(omega, receiver_x, receiver_f, 0, 0, COARSE)
+    for j in range(1, PAIRS):
+        p = j - side if j % 2 else j + side
         fill_pair(receiver_f, receiver, p)
         part = spread(p, slice(0, 2 * shots))
         for h in range(2):
@@ -225,7 +228,7 @@
             send(p, h)
 
     loads[2].wait()
-    fill_factors(omega, source_x, source_f, 0, FINE + COARSE)
+    fill_factors(omega, source_x, source_f, FINE, 0, COARSE)
     for p in range(PAIRS):
         fill_pair(source_f, source, p)
     mine[...] = source[:, own_rows].T

time: 66.1 us -> 65.1 us (0.985)
  Pallas kernels: 61.8 us -> 60.4 us
    pallas_call x1, Pallas kernels: 61.8 us -> 60.4 us  [one_frequency_fused(): pl.pallas_call(functools.partial(whole_kernel, first_hertz), out_shape=(j...]
where the time goes in v3:
time: 65.1 us; the launch traced here: 64.1 us
  Pallas kernels  60.4 us (93%)
  matrix products  3.66 us (6%)
    pallas_call x1, Pallas kernels, one_frequency_fused(): pl.pallas_call(functools.partial(whole_kernel, first_hertz), out_shape=(j...  60.4 us
    dot_general x1, matrix products, dot(): return jnp.dot(left, right, preferred_element_type=jnp.float32)  3.66 us

profile of v3, /device:TPU:0, one launch (start us, length us, event | category | flops | bytes accessed | tf_op | source)
XLA Modules:
  0.0 64.1 jit_solution(12489978020997492585)
XLA Ops:
  0.0 60.4 %plane_wave_multiples.1 = (bf16[512,1024]{1,0:T(8,128)(2,1)S(1)}, bf16[1024,2048]{1,0:T(8,128)(2,1)S(1)}) custom-call(bf16[512,2048]{1,0:T(8,128)(2,1)} %bitcast.8, f32[1,2048]{1,0:T(1,128)} %bitcast.9, f32[1,2048]{1,0:T(1,128)} %bitcast.10), custom_call_target="tpu_custom_call" | custom-call | tf_op jit(solution)/shard_map/plane_wave_multiples/pallas_call | solution.py:388
  60.5 3.7 %multiply_convert_fusion = bf16[512,2048]{1,0:T(8,128)(2,1)} fusion(bf16[512,1024]{1,0:T(8,128)(2,1)S(1)} %get-tuple-element.7, bf16[1024,2048]{1,0:T(8,128)(2,1)S(1)} %get-tuple-element.8), kind=kOutput, calls=%fused_computation | convolution fusion | flops 2149580800 | bytes 7340032 | tf_op jit(solution)/shard_map/dot_general | solution.py:128

commit v4 on v3

--- a/solution.py
+++ b/solution.py
@@ -68,6 +68,12 @@
     (2, 6, 1, 0, 5, 4, 3, 7),
     (1, 5, 2, 3, 6, 7, 0, 4),
     (3, 1, 7, 5, 2, 6, 0, 4),
+)
+SENDING = (
+    (0, 1, 2, 3, 4, 5, 6, 7),
+    (0, 1, 4, 3, 5, 7, 2, 6),
+    (2, 3, 0, 7, 6, 4, 1, 5),
+    (2, 3, 0, 1, 6, 7, 4, 5),
 )
 BLOCKS = len(OWNER)
 
@@ -129,8 +135,9 @@
 
 
 def whole_kernel(
-    first_hertz, data_in, receiver_in, source_in, back, receiver,
-    data, receiver_x, source_x, source, receiver_f, source_f, mine, outgoing, met, planes, half_way, total,
+    first_hertz, data_in, receiver_in, source_in, result, last_left, last_right,
+    data, receiver_x, source_x, receiver, source, receiver_f, source_f, mine, outgoing, met, planes, half_way,
+    total, back, crossed,
     spread_send, spread_recv, plane_send, plane_recv, twin_recv, load_sem,
 ):
     chips, cores = len(OWN), 2
@@ -149,9 +156,16 @@
         return out
 
     packed = pick([sum(nb << (3 * i) for i, nb in enumerate(row)) for row in ORDER])
+    sending = pick([sum(nb << (3 * i) for i, nb in enumerate(row)) for row in SENDING])
 
     def nth(i):
         return lax.rem(packed >> (3 * i), BLOCKS)
+
+    def owner_of(nb):
+        return 2 * lax.rem(nb, 2) + lax.rem(nb // 2, 2)
+
+    def block_rows(nb):
+        return pl.ds(pl.multiple_of(nb * BLOCK, BLOCK), BLOCK)
 
     def place(d):
         return {"shot": d // cores, "rep": d % cores}
@@ -172,67 +186,69 @@
     omega = two_pi * (base_hertz + step_hertz * hertz)
     own_rows = pl.ds(pl.multiple_of(me * shots, shots), shots)
 
-    def spread_copy(p, s, h, to):
-        return pltpu.make_async_remote_copy(
-            src_ref=outgoing.at[4 * p + 2 * s + h], dst_ref=met.at[p, own_rows],
-            send_sem=spread_send, recv_sem=spread_recv.at[p],
-            device_id={"shot": to, "rep": h}, device_id_type=MESH,
-        )
-
-    def put(p, h, part):
+    def put(blocks, h, part):
         part = (part * math.sqrt(2.0 / data.shape[1])).astype(jnp.bfloat16)
-        for s in range(2):
+        for s, nb in enumerate(blocks):
             piece = part[:, s * BLOCK : (s + 1) * BLOCK]
-            here = me == (2 * s + lax.rem(p, 2)) * cores + h
+            here = me == owner_of(nb) * cores + h
 
             @pl.when(here)
             def _():
-                met[p, own_rows, :] = piece
+                met[nb // 2, own_rows, :] = piece
 
             @pl.when(jnp.logical_not(here))
             def _():
-                outgoing[4 * p + 2 * s + h] = piece
-
-    def send(p, h):
+                outgoing[2 * nb + h] = piece
+
+    def send(blocks, h):
         for k in range(2):
-            s = lax.rem(1 - side + c + k, 2)
-            to = 2 * s + lax.rem(p, 2)
+            nb = jnp.where(lax.rem(1 - side + c + k, 2) == 0, *blocks)
+            to = owner_of(nb)
 
             @pl.when((to != z) | (c != h))
             def _():
-                spread_copy(p, s, h, to).start()
-
-    def spread(p, rows):
-        return lax.dot_general(
-            data[rows, :], receiver[pl.ds(pl.multiple_of(2 * BLOCK * p, 2 * BLOCK), 2 * BLOCK), :], (((1,), (1,)), ((), ())),
-            preferred_element_type=jnp.float32,
-        )
+                pltpu.make_async_remote_copy(
+                    src_ref=outgoing.at[2 * nb + h], dst_ref=met.at[nb // 2, own_rows],
+                    send_sem=spread_send, recv_sem=spread_recv.at[nb // 2],
+                    device_id={"shot": to, "rep": h}, device_id_type=MESH,
+                ).start()
+
+    def spread(blocks, rows):
+        right = jnp.concatenate([receiver[block_rows(nb), :] for nb in blocks], axis=0)
+        return lax.dot_general(data[rows, :], right, (((1,), (1,)), ((), ())), preferred_element_type=jnp.float32)
 
     loads[0].wait()
     fill_factors(omega, receiver_x, receiver_f, FINE, side * coarse, coarse)
     fill_pair(receiver_f, receiver, side)
     loads[1].wait()
-    for h in range(2):
-        put(side, h, spread(side, slice(h * shots, (h + 1) * shots)))
-        if h == 0:
-            pl.semaphore_wait(barrier, group - 1)
-        send(side, h)
-    fill_factors(omega, receiver_x, receiver_f, 0, 0, COARSE)
-    for j in range(1, PAIRS):
-        p = j - side if j % 2 else j + side
-        fill_pair(receiver_f, receiver, p)
-        part = spread(p, slice(0, 2 * shots))
+    for step in range(PAIRS):
+        blocks = [lax.rem(sending >> (3 * i), BLOCKS) for i in (2 * step, 2 * step + 1)]
+        if step == 0:
+            for h in range(2):
+                put(blocks, h, spread(blocks, slice(h * shots, (h + 1) * shots)))
+                if h == 0:
+                    pl.semaphore_wait(barrier, group - 1)
+                send(blocks, h)
+            fill_factors(omega, receiver_x, receiver_f, 0, 0, COARSE)
+            fill_pair(receiver_f, receiver, 1 - side)
+            fill_pair(receiver_f, receiver, 2 + side)
+            continue
+        part = spread(blocks, slice(0, 2 * shots))
         for h in range(2):
-            put(p, h, part[h * shots : (h + 1) * shots])
+            put(blocks, h, part[h * shots : (h + 1) * shots])
         for h in range(2):
-            send(p, h)
+            send(blocks, h)
+        if step == 1:
+            fill_pair(receiver_f, receiver, 3 - side)
 
     loads[2].wait()
     fill_factors(omega, source_x, source_f, FINE, 0, COARSE)
     for p in range(PAIRS):
         fill_pair(source_f, source, p)
     mine[...] = source[:, own_rows].T
-    half_way[...] = jnp.zeros_like(half_way)
+    for ref in (half_way, back, crossed, last_left, last_right):
+        ref[...] = jnp.zeros_like(ref)
+    outer = (z == 0) | (z == chips - 1)
 
     rows_of = NSLOW // PIECES
 
@@ -330,16 +346,53 @@
         back[:shots, columns(nb)] = (parts[0] * math.sqrt(1.0 / NSLOW)).astype(jnp.bfloat16)
         back[shots:, columns(nb)] = (parts[1] * math.sqrt(1.0 / NSLOW)).astype(jnp.bfloat16)
 
-    def add_late(n, keep, unroll):
+    def add_late(n, keep, keep_new):
         late = nth(n)
+        for i in range(n):
+            keep(nth(i), back_more(nth(i), late))
+        keep_new(late, back_new(late))
+
+    scale_back = math.sqrt(1.0 / NSLOW)
+    rec_count = receiver.shape[1]
+    tile = math.gcd(rec_count, 512)
+    last, before = BLOCKS - 1, BLOCKS - 2
+
+    def lanes_of(i):
+        return pl.ds(pl.multiple_of(i * tile, tile), tile)
+
+    def right_side():
+        late = nth(last)
+        for i in range(before):
+            for h in range(2):
+                crossed[h * BLOCK : (h + 1) * BLOCK, columns(nth(i))] = planes[nth(i), h, columns(late), :]
+        last_right[2 * BLOCK : 3 * BLOCK, :] = receiver[columns(late), :]
+        last_right[3 * BLOCK :, :] = receiver[columns(nth(before)), :]
 
         def step(i, carry):
-            keep(nth(i), back_more(nth(i), late))
+            part = dot(crossed[...], receiver[:, lanes_of(i)])
+            last_right[: 2 * BLOCK, lanes_of(i)] = (part * scale_back).astype(jnp.bfloat16)
             return carry
 
-        if n > 0:
-            lax.fori_loop(0, n, step, 0, unroll=unroll)
-        keep(late, back_new(late))
+        lax.fori_loop(0, rec_count // tile, step, 0)
+
+    def left_side():
+        late = nth(last)
+        half_slice(late)
+        real, imaginary = half_way[:shots, columns(late)], half_way[shots:, columns(late)]
+        last_left[:shots, :BLOCK] = real
+        last_left[:shots, BLOCK : 2 * BLOCK] = -imaginary
+        last_left[shots:, :BLOCK] = imaginary
+        last_left[shots:, BLOCK : 2 * BLOCK] = real
+        for at, parts in ((2, back_new(late)), (3, back_more(nth(before), late))):
+            for rows, part in zip((slice(0, shots), slice(shots, 2 * shots)), parts):
+                last_left[rows, at * BLOCK : (at + 1) * BLOCK] = (part * scale_back).astype(jnp.bfloat16)
+
+    def result_so_far():
+        def step(i, carry):
+            result[:, lanes_of(i)] = dot(back[...], receiver[:, lanes_of(i)])
+            return carry
+
+        lax.fori_loop(0, rec_count // tile, step, 0)
 
     for i in range(BLOCKS):
         nb = nth(i)
@@ -353,20 +406,48 @@
             @pl.when(jnp.logical_not(mine_now))
             def _():
                 passed_slice(i, nb)
-        if 0 < i < BLOCKS - 1:
+        if 0 < i < before:
             half_slice(nth(i - 1))
-            add_late(i - 1, keep_total, 1)
-        if i == BLOCKS - 2:
+            add_late(i - 1, keep_total, keep_total)
+        if i == before - 1:
+            @pl.when(outer)
+            def _():
+                half_slice(nb)
+                add_late(i, keep_total, keep_total)
+                right_side()
+        if i == before:
+            @pl.when(jnp.logical_not(outer))
+            def _():
+                half_slice(nth(i - 1))
+                add_late(i - 1, keep_total, keep_total)
+
             half_slice(nb)
-            add_late(i, keep_total, 1)
+
+            @pl.when(outer)
+            def _():
+                add_late(i, keep_back, keep_total)
+                result_so_far()
+
+            @pl.when(jnp.logical_not(outer))
+            def _():
+                add_late(i, keep_total, keep_total)
 
     sent = outgoing.at[pl.ds(0, 2 * BLOCKS - len(OWN[0]))]
     pltpu.make_async_remote_copy(
         src_ref=sent, dst_ref=sent, send_sem=spread_send, recv_sem=spread_recv.at[0],
         device_id={"rep": 1 - c}, device_id_type=MESH,
     ).wait_send()
-    half_slice(nth(BLOCKS - 1))
-    add_late(BLOCKS - 1, keep_back, True)
+
+    @pl.when(outer)
+    def _():
+        left_side()
+
+    @pl.when(jnp.logical_not(outer))
+    def _():
+        half_slice(nth(last))
+        add_late(last, keep_back, keep_back)
+        result_so_far()
+
     for at in range(chips):
         counts = [sum(owner <= at for owner in OWNER), sum(owner >= at for owner in OWNER)]
 
@@ -385,18 +466,20 @@
     group = 2 * len(OWN)
     vmem = pl.BlockSpec(memory_space=pltpu.VMEM)
     half = jnp.bfloat16
-    back, receiver = pl.pallas_call(
+    total, left, right = pl.pallas_call(
         functools.partial(whole_kernel, first_hertz),
         out_shape=(
-            jax.ShapeDtypeStruct((2 * shots, NSLOW), half),
-            jax.ShapeDtypeStruct((NSLOW, rec_count), half),
+            jax.ShapeDtypeStruct((2 * shots, rec_count), jnp.float32),
+            jax.ShapeDtypeStruct((2 * shots, 4 * BLOCK), half),
+            jax.ShapeDtypeStruct((4 * BLOCK, rec_count), half),
         ),
         in_specs=[pl.BlockSpec(memory_space=pltpu.HBM)] * 3,
-        out_specs=(vmem, vmem),
+        out_specs=(vmem, vmem, vmem),
         scratch_shapes=[
             pltpu.VMEM((2 * shots, rec_count), half),
             pltpu.VMEM((1, rec_count), jnp.float32),
             pltpu.VMEM((1, src_count), jnp.float32),
+            pltpu.VMEM((NSLOW, rec_count), half),
             pltpu.VMEM((NSLOW, src_count), half),
             pltpu.VMEM((2, COARSE + FINE, rec_count), jnp.float32),
             pltpu.VMEM((2, COARSE + FINE, src_count), jnp.float32),
@@ -406,6 +489,8 @@
             pltpu.VMEM((BLOCKS, 2, NSLOW, BLOCK), half),
             pltpu.VMEM((2 * shots, NSLOW), half),
             pltpu.VMEM((BLOCKS, 2 * shots, BLOCK), jnp.float32),
+            pltpu.VMEM((2 * shots, NSLOW), half),
+            pltpu.VMEM((2 * BLOCK, NSLOW), half),
             pltpu.SemaphoreType.DMA,
             pltpu.SemaphoreType.DMA((PAIRS,)),
             pltpu.SemaphoreType.DMA((3,)),
@@ -421,7 +506,7 @@
         pltpu.with_memory_space_constraint(x, pltpu.HBM)
         for x in (data.reshape(2 * shots, rec_count), receiver_x.reshape(1, rec_count), source_x.reshape(1, src_count))
     ])
-    result = (dot(back, receiver) * math.sqrt(2.0 / NSLOW)).astype(half)
+    result = ((dot(left, right) + total) * math.sqrt(2.0 / NSLOW)).astype(half)
     return result.reshape(2, shots, rec_count)
 
 

time: 65.1 us -> 62.8 us (0.965); the launches traced: 64.1 us -> 62.6 us
  matrix products: 3.66 us -> 2.6 us
    dot_general x1, matrix products: 3.66 us -> 2.6 us  [dot(): return jnp.dot(left, right, preferred_element_type=jnp.float32)]
where the time goes in v4:
time: 62.8 us; the launch traced here: 62.6 us
  Pallas kernels  60 us (96%)
  matrix products  2.6 us (4%)
    pallas_call x1, Pallas kernels, one_frequency_fused(): pl.pallas_call(functools.partial(whole_kernel, first_hertz), out_shape=(j...  60 us
    dot_general x1, matrix products, dot(): return jnp.dot(left, right, preferred_element_type=jnp.float32)  2.6 us

profile of v4, /device:TPU:0, one launch (start us, length us, event | category | flops | bytes accessed | tf_op | source)
XLA Modules:
  0.0 62.6 jit_solution(5146301132674905120)
XLA Ops:
  0.0 60.0 %plane_wave_multiples.1 = (f32[512,2048]{1,0:T(8,128)S(1)}, bf16[512,512]{1,0:T(8,128)(2,1)S(1)}, bf16[512,2048]{1,0:T(8,128)(2,1)S(1)}) custom-call(bf16[512,2048]{1,0:T(8,128)(2,1)} %bitcast.8, f32[1,2048]{1,0:T(1,128)} %bitcast.9, f32[1,2048]{1,0:T(1,128)} %bitcast.10), custom_call_target="tpu_custom_call" | custom-call | tf_op jit(solution)/shard_map/plane_wave_multiples/pallas_call | solution.py:469
  60.0 2.6 %multiply_convert_fusion = bf16[512,2048]{1,0:T(8,128)(2,1)} fusion(f32[512,2048]{1,0:T(8,128)S(1)} %get-tuple-element.10, bf16[512,512]{1,0:T(8,128)(2,1)S(1)} %get-tuple-element.8, bf16[512,2048]{1,0:T(8,128)(2,1)S(1)} %get-tuple-element.9), kind=kOutput, calls=%fused_computation | convolution fusion | flops 1076887552 | bytes 8912896 | tf_op jit(solution)/shard_map/dot_general | solution.py:134

commit v5 on v4

--- a/solution.py
+++ b/solution.py
@@ -376,14 +376,28 @@
         lax.fori_loop(0, rec_count // tile, step, 0)
 
     def left_side():
-        late = nth(last)
-        half_slice(late)
-        real, imaginary = half_way[:shots, columns(late)], half_way[shots:, columns(late)]
+        late, old = nth(last), nth(before)
+        whole_copy(2, pl.ds(late, 1), twin_recv.at[late]).wait_recv()
+        both = jnp.concatenate([planes[late, 0], planes[late, 1]], axis=1)
+        sign = (1 - 2 * lax.rem(late, 2)).astype(jnp.float32) * math.sqrt(2.0 / NSLOW)
+        part = (dot(mine[...], both) * sign).astype(jnp.bfloat16)
+        base = dot(half_way[...], both)
+        real, imaginary = part[:, :BLOCK], part[:, BLOCK:]
+        top = jnp.concatenate([real, imaginary], axis=0)
         last_left[:shots, :BLOCK] = real
         last_left[:shots, BLOCK : 2 * BLOCK] = -imaginary
         last_left[shots:, :BLOCK] = imaginary
         last_left[shots:, BLOCK : 2 * BLOCK] = real
-        for at, parts in ((2, back_new(late)), (3, back_more(nth(before), late))):
+
+        def rest(nb):
+            rows = jnp.concatenate([planes[nb, 0, columns(late), :], planes[nb, 1, columns(late), :]], axis=1)
+            return dot(top, rows)
+
+        parts = mix(rest(old))
+        for at, parts in (
+            (3, (total[old, :shots] + parts[0], total[old, shots:] + parts[1])),
+            (2, mix(base + rest(late))),
+        ):
             for rows, part in zip((slice(0, shots), slice(shots, 2 * shots)), parts):
                 last_left[rows, at * BLOCK : (at + 1) * BLOCK] = (part * scale_back).astype(jnp.bfloat16)
 
@@ -438,6 +452,15 @@
         device_id={"rep": 1 - c}, device_id_type=MESH,
     ).wait_send()
 
+    for at in range(chips):
+        counts = [sum(owner <= at for owner in OWNER), sum(owner >= at for owner in OWNER)]
+
+        @pl.when(z == at)
+        def _():
+            for way, count in enumerate(counts):
+                if count < BLOCKS:
+                    whole_copy(way, pl.ds(0, count), twin_recv.at[0]).wait_send()
+
     @pl.when(outer)
     def _():
         left_side()
@@ -448,16 +471,21 @@
         add_late(last, keep_back, keep_back)
         result_so_far()
 
-    for at in range(chips):
-        counts = [sum(owner <= at for owner in OWNER), sum(owner >= at for owner in OWNER)]
-
-        @pl.when(z == at)
-        def _():
-            for way, count in enumerate(counts):
-                if count < BLOCKS:
-                    whole_copy(way, pl.ds(0, count), twin_recv.at[0]).wait_send()
-
     whole_copy(2, pl.ds(0, BLOCKS), twin_recv.at[0]).wait_send()
+
+
+def finish_kernel(total, left, right, out, staged, sems):
+    rec_count = total.shape[1]
+    tile = math.gcd(rec_count, 256)
+    copies = []
+    for i in range(rec_count // tile):
+        lanes = slice(i * tile, (i + 1) * tile)
+        part = (dot(left[...], right[:, lanes]) + total[:, lanes]) * math.sqrt(2.0 / NSLOW)
+        staged[:, lanes] = part.astype(jnp.bfloat16)
+        copies.append(pltpu.make_async_copy(staged.at[:, lanes], out.at[:, lanes], sems.at[i]))
+        copies[-1].start()
+    for copy in copies:
+        copy.wait()
 
 
 def one_frequency_fused(first_hertz, data, receiver_x, source_x):
@@ -506,7 +534,18 @@
         pltpu.with_memory_space_constraint(x, pltpu.HBM)
         for x in (data.reshape(2 * shots, rec_count), receiver_x.reshape(1, rec_count), source_x.reshape(1, src_count))
     ])
-    result = ((dot(left, right) + total) * math.sqrt(2.0 / NSLOW)).astype(half)
+    result = pl.pallas_call(
+        finish_kernel,
+        out_shape=jax.ShapeDtypeStruct((2 * shots, rec_count), half),
+        in_specs=[vmem] * 3,
+        out_specs=pl.BlockSpec(memory_space=pl.ANY),
+        scratch_shapes=[
+            pltpu.VMEM((2 * shots, rec_count), half),
+            pltpu.SemaphoreType.DMA((rec_count // math.gcd(rec_count, 256),)),
+        ],
+        compiler_params=pltpu.CompilerParams(vmem_limit_bytes=24 * 1024 * 1024),
+        name="last_block",
+    )(total, left, right)
     return result.reshape(2, shots, rec_count)
 
 

time: 62.8 us -> 62.6 us (level)
  matrix products: 2.6 us -> 0 us
  Pallas kernels: 60 us -> 62.2 us
    dot_general x1 -> x0, matrix products: 2.6 us -> none  [dot(): return jnp.dot(left, right, preferred_element_type=jnp.float32)]
    pallas_call x0 -> x1, Pallas kernels: none -> 2.2 us  [one_frequency_fused(): pl.pallas_call(finish_kernel, out_shape=jax.ShapeDtypeStruct((2 * shots,...]
where the time goes in v5:
time: 62.6 us; the launch traced here: 62.4 us
  Pallas kernels  62.2 us (99%)
    pallas_call x1, Pallas kernels, one_frequency_fused(): pl.pallas_call(functools.partial(whole_kernel, first_hertz), out_shape=(j...  60 us
    pallas_call x1, Pallas kernels, one_frequency_fused(): pl.pallas_call(finish_kernel, out_shape=jax.ShapeDtypeStruct((2 * shots,...  2.2 us

profile of v5, /device:TPU:0, one launch (start us, length us, event | category | flops | bytes accessed | tf_op | source)
XLA Modules:
  0.0 62.4 jit_solution(8885769618348540661)
XLA Ops:
  0.0 60.0 %plane_wave_multiples.1 = (f32[512,2048]{1,0:T(8,128)S(1)}, bf16[512,512]{1,0:T(8,128)(2,1)S(1)}, bf16[512,2048]{1,0:T(8,128)(2,1)S(1)}) custom-call(bf16[512,2048]{1,0:T(8,128)(2,1)} %bitcast.6, f32[1,2048]{1,0:T(1,128)} %bitcast.7, f32[1,2048]{1,0:T(1,128)} %bitcast.8), custom_call_target="tpu_custom_call" | custom-call | tf_op jit(solution)/shard_map/plane_wave_multiples/pallas_call | solution.py:497
  60.0 2.2 %last_block.1 = bf16[512,2048]{1,0:T(8,128)(2,1)} custom-call(f32[512,2048]{1,0:T(8,128)S(1)} %get-tuple-element.8.total, bf16[512,512]{1,0:T(8,128)(2,1)S(1)} %get-tuple-element.9.left, bf16[512,2048]{1,0:T(8,128)(2,1)S(1)} %get-tuple-element.10.right), custom_call_target="tpu_custom_call" | custom-call | tf_op jit(solution)/shard_map/last_block/pallas_call | solution.py:537

commit v6 on v5

--- a/solution.py
+++ b/solution.py
@@ -70,10 +70,10 @@
     (3, 1, 7, 5, 2, 6, 0, 4),
 )
 SENDING = (
-    (0, 1, 2, 3, 4, 5, 6, 7),
-    (0, 1, 4, 3, 5, 7, 2, 6),
-    (2, 3, 0, 7, 6, 4, 1, 5),
-    (2, 3, 0, 1, 6, 7, 4, 5),
+    (0, 1, 2, 3, 6, 7, 4, 5),
+    (0, 1, 4, 3, 2, 6, 5, 7),
+    (2, 3, 0, 7, 1, 5, 6, 4),
+    (2, 3, 0, 1, 4, 5, 6, 7),
 )
 BLOCKS = len(OWNER)
 

time: 62.6 us -> 62.6 us (level)
  no operation moved by 1% of the time
where the time goes in v6:
time: 62.6 us; the launch traced here: 62.4 us
  Pallas kernels  62.2 us (99%)
    pallas_call x1, Pallas kernels, one_frequency_fused(): pl.pallas_call(functools.partial(whole_kernel, first_hertz), out_shape=(j...  60 us
    pallas_call x1, Pallas kernels, one_frequency_fused(): pl.pallas_call(finish_kernel, out_shape=jax.ShapeDtypeStruct((2 * shots,...  2.2 us

profile of v6, /device:TPU:0, one launch (start us, length us, event | category | flops | bytes accessed | tf_op | source)
XLA Modules:
  0.0 62.4 jit_solution(3868398058755030713)
XLA Ops:
  0.0 60.0 %plane_wave_multiples.1 = (f32[512,2048]{1,0:T(8,128)S(1)}, bf16[512,512]{1,0:T(8,128)(2,1)S(1)}, bf16[512,2048]{1,0:T(8,128)(2,1)S(1)}) custom-call(bf16[512,2048]{1,0:T(8,128)(2,1)} %bitcast.6, f32[1,2048]{1,0:T(1,128)} %bitcast.7, f32[1,2048]{1,0:T(1,128)} %bitcast.8), custom_call_target="tpu_custom_call" | custom-call | tf_op jit(solution)/shard_map/plane_wave_multiples/pallas_call | solution.py:497
  60.0 2.2 %last_block.1 = bf16[512,2048]{1,0:T(8,128)(2,1)} custom-call(f32[512,2048]{1,0:T(8,128)S(1)} %get-tuple-element.8.total, bf16[512,512]{1,0:T(8,128)(2,1)S(1)} %get-tuple-element.9.left, bf16[512,2048]{1,0:T(8,128)(2,1)S(1)} %get-tuple-element.10.right), custom_call_target="tpu_custom_call" | custom-call | tf_op jit(solution)/shard_map/last_block/pallas_call | solution.py:537

commit v7 on v5

--- a/solution.py
+++ b/solution.py
@@ -403,7 +403,7 @@
 
     def result_so_far():
         def step(i, carry):
-            result[:, lanes_of(i)] = dot(back[...], receiver[:, lanes_of(i)])
+            result[:, lanes_of(i)] = dot(back[...], receiver[:, lanes_of(i)]).astype(jnp.bfloat16)
             return carry
 
         lax.fori_loop(0, rec_count // tile, step, 0)
@@ -497,7 +497,7 @@
     total, left, right = pl.pallas_call(
         functools.partial(whole_kernel, first_hertz),
         out_shape=(
-            jax.ShapeDtypeStruct((2 * shots, rec_count), jnp.float32),
+            jax.ShapeDtypeStruct((2 * shots, rec_count), half),
             jax.ShapeDtypeStruct((2 * shots, 4 * BLOCK), half),
             jax.ShapeDtypeStruct((4 * BLOCK, rec_count), half),
         ),

time: 62.6 us -> 62.5 us (level)
  no operation moved by 1% of the time
where the time goes in v7:
time: 62.5 us; the launch traced here: 62.4 us
  Pallas kernels  62.2 us (100%)
    pallas_call x1, Pallas kernels, one_frequency_fused(): pl.pallas_call(functools.partial(whole_kernel, first_hertz), out_shape=(j...  60 us
    pallas_call x1, Pallas kernels, one_frequency_fused(): pl.pallas_call(finish_kernel, out_shape=jax.ShapeDtypeStruct((2 * shots,...  2.2 us

profile of v7, /device:TPU:0, one launch (start us, length us, event | category | flops | bytes accessed | tf_op | source)
XLA Modules:
  0.0 62.4 jit_solution(18328003408900941712)
XLA Ops:
  0.0 60.0 %plane_wave_multiples.1 = (bf16[512,2048]{1,0:T(8,128)(2,1)S(1)}, bf16[512,512]{1,0:T(8,128)(2,1)S(1)}, bf16[512,2048]{1,0:T(8,128)(2,1)S(1)}) custom-call(bf16[512,2048]{1,0:T(8,128)(2,1)} %bitcast.6, f32[1,2048]{1,0:T(1,128)} %bitcast.7, f32[1,2048]{1,0:T(1,128)} %bitcast.8), custom_call_target="tpu_custom_call" | custom-call | tf_op jit(solution)/shard_map/plane_wave_multiples/pallas_call | solution.py:497
  60.0 2.2 %last_block.1 = bf16[512,2048]{1,0:T(8,128)(2,1)} custom-call(bf16[512,2048]{1,0:T(8,128)(2,1)S(1)} %get-tuple-element.8.total, bf16[512,512]{1,0:T(8,128)(2,1)S(1)} %get-tuple-element.9.left, bf16[512,2048]{1,0:T(8,128)(2,1)S(1)} %get-tuple-element.10.right), custom_call_target="tpu_custom_call" | custom-call | tf_op jit(solution)/shard_map/last_block/pallas_call | solution.py:537
